TPU v7x, 128 devices: a whole 4x4x4 slice. The times are simulated.
128 devices in a mesh: seq: 32 (over y_lo, z, x), head: 4 (over y_hi, core).
Axes of the slice: x: 4, y: 4 (y_hi: 2, y_lo: 2; y = y_hi * 2 + y_lo), z: 4, core: 2. Of those that a mesh axis runs over, the one named last changes fastest.
Arguments:
- queries: bfloat16 [4096, 3072], P('seq', 'head'), may hold values from -8 to 8
- latents: bfloat16 [4096, 576], P('seq'), may hold values from -8 to 8
- key_up: bfloat16 [512, 2048], P(None, 'head'), may hold values from -0.25 to 0.25
- value_up: bfloat16 [512, 2048], P(None, 'head'), may hold values from -0.25 to 0.25
- out_grad: bfloat16 [4096, 2048], P('seq', 'head'), may hold values from -48 to 48
- positions: int32 [4096], P('seq'), may hold values from 0 to 4095, as said below
Outputs:
- query_grad: bfloat16 [4096, 3072], P('seq', 'head')
- latent_grad: float32 [4096, 576], P('seq')
- key_up_grad: float32 [512, 2048], P(None, 'head')
- value_up_grad: float32 [512, 2048], P(None, 'head')
Inputs may be any that keep to these rules, and one draw needn't show every extreme that they name: Every position from 0 to 4095 occurs once; positions come in stripes of 128 consecutive positions in ascending order, each stripe whole within the rows of one device.
All inputs are finite; a program needn't handle non-finite values.
Results may differ from a plain program's by a relative error of at most 0.0084.
Values may be sent and summed in bfloat16 or wider, within the bound.
A program may use at most 64 MiB of HBM per device.

v0:
```python
import math
import jax
import jax.numpy as jnp
from jax import lax
from jax.sharding import PartitionSpec as P

D_LAT = 512
D_ROPE = 64
D_NOPE = 128
D_V = 128
NEG = -1e30


def joined_along(tiles, dim):
    tiles = jnp.moveaxis(tiles, 0, dim)
    dims = tiles.shape
    return tiles.reshape(*dims[:dim], dims[dim] * dims[dim + 1], *dims[dim + 2 :])


def from_everyone(shard, axis):
    size = lax.axis_size(axis)
    return lax.all_to_all(
        jnp.broadcast_to(shard[None], (size, *shard.shape)), axis, 0, 0, tiled=True
    )


def collect(shard, axis, dim):
    return joined_along(from_everyone(shard, axis), dim)


def shifted(value, axis, steps):
    count = lax.axis_size(axis)
    pairs = [(source, (source + steps) % count) for source in range(count)]
    return lax.ppermute(value, axis, pairs)


def taken_together(shard, axis):
    return from_everyone(shard, axis).sum(axis=0)


def cut_along(shard, dim, size):
    before, after = (shard.shape[:dim], shard.shape[dim + 1 :])
    return jnp.moveaxis(shard.reshape(*before, size, -1, *after), dim, 0)


def summed_on_arrival(shard, axis, dim):
    tiles = cut_along(shard, dim, lax.axis_size(axis))
    arrived = lax.all_to_all(tiles, axis, split_axis=0, concat_axis=0, tiled=True)
    return arrived.sum(axis=0)


def filled_up(lines, size):
    spare = -len(lines) % size
    return jnp.pad(lines, [(0, spare)] + [(0, 0)] * (lines.ndim - 1))


def sum_by_parts(shard, axes):
    own = summed_on_arrival(filled_up(shard, lax.axis_size(axes)), axes, 0)
    whole = collect(own, axes, 0)
    return whole[: len(shard)].reshape(shard.shape)


def together(arrays, axis):
    vector, at, done = (jnp.concatenate([a.reshape(-1) for a in arrays]), 0, [])
    so_far = sum_by_parts(vector, axis)
    for a in arrays:
        done.append(so_far[at : at + a.size].reshape(a.shape))
        at += a.size
    return tuple(done)


def up_project(block, key_up, value_up):
    compressed = block[:, :D_LAT]
    key_nope = jnp.dot(compressed, key_up, preferred_element_type=jnp.float32).astype(jnp.bfloat16)
    values = jnp.dot(compressed, value_up, preferred_element_type=jnp.float32).astype(jnp.bfloat16)
    return (key_nope, block[:, D_LAT:], values)


def split_heads(queries, out_grad, key_nope, values):
    heads = key_nope.shape[1] // D_NOPE
    shaped = queries.reshape(queries.shape[0], heads, D_NOPE + D_ROPE)
    grads = out_grad.reshape(out_grad.shape[0], heads, D_V)
    key3 = key_nope.reshape(key_nope.shape[0], heads, D_NOPE)
    value3 = values.reshape(values.shape[0], heads, D_V)
    return (shaped[:, :, :D_NOPE], shaped[:, :, D_NOPE:], grads, key3, value3)


def scores_of(q_nope, q_rope, key3, rope_keys, query_pos, key_pos):
    scale = 1.0 / math.sqrt(D_NOPE + D_ROPE)
    raw = jnp.einsum("bhd,khd->hbk", q_nope, key3, preferred_element_type=jnp.float32)
    raw = raw + jnp.einsum("bhd,kd->hbk", q_rope, rope_keys, preferred_element_type=jnp.float32)
    visible = (key_pos[None, :] <= query_pos[:, None])[None]
    return (raw * scale, visible)


def forward_update(stats, queries, out_grad, query_pos, key_nope, rope_keys, values, key_pos):
    top, total, weighted = stats
    q_nope, q_rope, grads, key3, value3 = split_heads(queries, out_grad, key_nope, values)
    scores, visible = scores_of(q_nope, q_rope, key3, rope_keys, query_pos, key_pos)
    dprobs = jnp.einsum("bhd,khd->hbk", grads, value3, preferred_element_type=jnp.float32)
    masked = jnp.where(visible, scores, NEG)
    new_top = jnp.maximum(top, jnp.max(masked, axis=2))
    weights = jnp.exp(jnp.where(visible, scores - new_top[:, :, None], NEG))
    fade = jnp.exp(top - new_top)
    total = total * fade + jnp.sum(weights, axis=2)
    weighted = weighted * fade + jnp.sum(weights * dprobs, axis=2)
    return (new_top, total, weighted)


def backward_terms(queries, out_grad, query_pos, lse, delta, key_nope, rope_keys, values, key_pos):
    scale = 1.0 / math.sqrt(D_NOPE + D_ROPE)
    q_nope, q_rope, grads, key3, value3 = split_heads(queries, out_grad, key_nope, values)
    scores, visible = scores_of(q_nope, q_rope, key3, rope_keys, query_pos, key_pos)
    probs = jnp.exp(jnp.where(visible, scores - lse[:, :, None], NEG))
    dprobs = jnp.einsum("bhd,khd->hbk", grads, value3, preferred_element_type=jnp.float32)
    dscore = (probs * (dprobs - delta[:, :, None]) * scale).astype(jnp.bfloat16)
    probs16 = probs.astype(jnp.bfloat16)
    grad_nope = jnp.einsum("hbk,khd->bhd", dscore, key3, preferred_element_type=jnp.float32)
    grad_rope = jnp.einsum("hbk,kd->bhd", dscore, rope_keys, preferred_element_type=jnp.float32)
    q_grad = jnp.concatenate([grad_nope, grad_rope], axis=2).reshape(queries.shape[0], -1)
    key_part = jnp.einsum("hbk,bhd->khd", dscore, q_nope, preferred_element_type=jnp.float32)
    value_part = jnp.einsum("hbk,bhd->khd", probs16, grads, preferred_element_type=jnp.float32)
    rope_part = jnp.einsum("hbk,bhd->kd", dscore, q_rope, preferred_element_type=jnp.float32)
    key_rows = key3.shape[0]
    part = jnp.concatenate(
        [key_part.reshape(key_rows, -1), value_part.reshape(key_rows, -1), rope_part], axis=1
    )
    return (q_grad, part)


def shards(queries, latents, key_up, value_up, out_grad, positions):
    rows = queries.shape[0]
    heads = key_up.shape[1] // D_NOPE
    qcols = queries.shape[1]
    nseq = lax.axis_size("seq")
    here = lax.axis_index("seq")
    every_pos = collect(positions, "seq", 0)
    part_width = heads * (D_NOPE + D_V) + D_ROPE

    def owner_start(step):
        return (here - step) % nseq * rows

    def owner_pos(step):
        return lax.dynamic_slice_in_dim(every_pos, owner_start(step), rows, 0)

    start_stats = (
        jnp.full((heads, rows), NEG, jnp.float32),
        jnp.zeros((heads, rows), jnp.float32),
        jnp.zeros((heads, rows), jnp.float32),
    )
    zero_grads = jnp.zeros((rows, part_width), jnp.float32)
    zero_query = jnp.zeros((rows, qcols), jnp.float32)

    def fold_block(stats, block, start):
        key_nope, rope_keys, values = up_project(block, key_up, value_up)
        key_pos = lax.dynamic_slice_in_dim(every_pos, start, block.shape[0], 0)
        return forward_update(
            stats, queries, out_grad, positions, key_nope, rope_keys, values, key_pos
        )

    def grad_block(block, grads, q_acc, step, lse, delta):
        key_nope, rope_keys, values = up_project(block, key_up, value_up)
        q_grad, part = backward_terms(
            queries, out_grad, positions, lse, delta, key_nope, rope_keys, values, owner_pos(step)
        )
        return (grads + part, q_acc + q_grad)

    gathered = lax.all_gather(latents, "seq", axis=0, tiled=True)
    count = gathered.shape[0]
    width = math.gcd(count, 512)

    def turn(index, carry):
        block = lax.dynamic_slice_in_dim(gathered, index * width, width, 0)
        return fold_block(carry, block, index * width)

    top, total, weighted = lax.fori_loop(0, count // width, turn, start_stats)
    lse = top + jnp.log(total)
    delta = weighted / total

    def kept_turn(step, carry):
        grads, q_acc = carry
        block = lax.dynamic_slice_in_dim(gathered, owner_start(step), rows, 0)
        grads, q_acc = grad_block(block, grads, q_acc, step, lse, delta)
        grads = shifted(grads, "seq", 1)
        return (grads, q_acc)

    grads, q_acc = lax.fori_loop(0, nseq - 1, kept_turn, (zero_grads, zero_query))
    last_block = lax.dynamic_slice_in_dim(gathered, owner_start(nseq - 1), rows, 0)
    grads, q_acc = grad_block(last_block, grads, q_acc, nseq - 1, lse, delta)
    key_grads = shifted(grads, "seq", 1)
    split_one = heads * D_NOPE
    split_two = split_one + heads * D_V
    key_grad = key_grads[:, :split_one]
    value_grad = key_grads[:, split_one:split_two]
    key_up32 = key_up.astype(jnp.float32)
    value_up32 = value_up.astype(jnp.float32)
    inner = (((1,), (1,)), ((), ()))
    folded = lax.dot_general(key_grad, key_up32, inner)
    folded = folded + lax.dot_general(value_grad, value_up32, inner)
    latent_part = jnp.concatenate([folded, key_grads[:, split_two:]], axis=1)
    latent_grad = taken_together(latent_part, "head")
    compressed = latents[:, :D_LAT].astype(jnp.float32)
    outer = (((0,), (0,)), ((), ()))
    key_term = lax.dot_general(compressed, key_grad, outer)
    value_term = lax.dot_general(compressed, value_grad, outer)
    key_up_grad, value_up_grad = together((key_term, value_term), "seq")
    return (q_acc.astype(jnp.bfloat16), latent_grad, key_up_grad, value_up_grad)


def solution(mesh):
    in_specs = (
        P("seq", "head"),
        P("seq", None),
        P(None, "head"),
        P(None, "head"),
        P("seq", "head"),
        P("seq"),
    )
    out_specs = (P("seq", "head"), P("seq", None), P(None, "head"), P(None, "head"))
    return jax.shard_map(shards, mesh=mesh, in_specs=in_specs, out_specs=out_specs, check_vma=False)
```

profile of v0, /device:TPU:0, one launch (start us, length us, event | category | flops | bytes accessed | tf_op | source)
XLA Modules:
  0.0 1031.5 jit_solution(13648473115734894433)
XLA Ops:
  28.9 123.4 %all-gather.2.cloned.1.call-done = bf16[4096,576]{0,1:T(8,128)(2,1)} async-done(((bf16[128,576]{0,1:T(8,128)(2,1)}), bf16[4096,576]{0,1:T(8,128)(2,1)}) %all-gather.2.cloned.1.call-update) | async-done | bytes 4718608 | tf_op jit(solution)/shard_map/all_gather | solution.py:168
  152.4 67.2 %while.36 = (s32[]{:T(128)}, f32[4,128]{1,0:T(4,128)S(1)}, f32[4,128]{1,0:T(4,128)S(1)}, f32[4,128]{1,0:T(4,128)}, s32[4096]{0:T(1024)}, /*index=5*/s32[128]{0:T...) while((s32[]{:T(128)}, f32[4,128]{1,0:T(4,128)S(1)}, ...), condition=%wide.region_4.5_spmd.clone, body=%wide.region_0.4_spmd.clone.sunk | while | flops 708120064 | bytes 10660626 | solution.py:176
  226.1 677.1 %while.37 = (s32[]{:T(128)}, f32[128,1088]{0,1:T(8,128)S(1)}, f32[128,768]{0,1:T(8,128)S(1)}, s32[]{:T(128)}, s32[4096]{0:T(1024)}, /*index=5*/s32[128]{0:T(128)...) while((s32[]{:T(128)}, f32[128,1088]{0,1:T(8,128)S(1)}, ...), condition=%wide.region_6.7_spmd.clone, body=%wide.region_5.6_spmd.clone.sunk | while | flops 244719632 | bytes 11737526 | solution.py:187
  233.8 15.9 %collective-permute-done = f32[128,1088]{0,1:T(8,128)S(1)} collective-permute-done((f32[128,1088]{0,1:T(8,128)}, f32[128,1088]{0,1:T(8,128)S(1)}, u32[]{:S(2)}, u32[]{:S(2)}) %collective-permute-start) | collective-permute-done | bytes 557088 | tf_op jit(solution)/shard_map/while/body/eval_jaxpr/ppermute | solution.py:34
  257.0 15.4 %collective-permute-done = f32[128,1088]{0,1:T(8,128)S(1)} collective-permute-done((f32[128,1088]{0,1:T(8,128)}, f32[128,1088]{0,1:T(8,128)S(1)}, u32[]{:S(2)}, u32[]{:S(2)}) %collective-permute-start) | collective-permute-done | bytes 557088 | tf_op jit(solution)/shard_map/while/body/eval_jaxpr/ppermute | solution.py:34
  279.7 14.5 %collective-permute-done = f32[128,1088]{0,1:T(8,128)S(1)} collective-permute-done((f32[128,1088]{0,1:T(8,128)}, f32[128,1088]{0,1:T(8,128)S(1)}, u32[]{:S(2)}, u32[]{:S(2)}) %collective-permute-start) | collective-permute-done | bytes 557088 | tf_op jit(solution)/shard_map/while/body/eval_jaxpr/ppermute | solution.py:34
  301.6 13.7 %collective-permute-done = f32[128,1088]{0,1:T(8,128)S(1)} collective-permute-done((f32[128,1088]{0,1:T(8,128)}, f32[128,1088]{0,1:T(8,128)S(1)}, u32[]{:S(2)}, u32[]{:S(2)}) %collective-permute-start) | collective-permute-done | bytes 557088 | tf_op jit(solution)/shard_map/while/body/eval_jaxpr/ppermute | solution.py:34
  322.6 12.8 %collective-permute-done = f32[128,1088]{0,1:T(8,128)S(1)} collective-permute-done((f32[128,1088]{0,1:T(8,128)}, f32[128,1088]{0,1:T(8,128)S(1)}, u32[]{:S(2)}, u32[]{:S(2)}) %collective-permute-start) | collective-permute-done | bytes 557088 | tf_op jit(solution)/shard_map/while/body/eval_jaxpr/ppermute | solution.py:34
  362.8 12.8 %collective-permute-done = f32[128,1088]{0,1:T(8,128)S(1)} collective-permute-done((f32[128,1088]{0,1:T(8,128)}, f32[128,1088]{0,1:T(8,128)S(1)}, u32[]{:S(2)}, u32[]{:S(2)}) %collective-permute-start) | collective-permute-done | bytes 557088 | tf_op jit(solution)/shard_map/while/body/eval_jaxpr/ppermute | solution.py:34
  382.9 12.8 %collective-permute-done = f32[128,1088]{0,1:T(8,128)S(1)} collective-permute-done((f32[128,1088]{0,1:T(8,128)}, f32[128,1088]{0,1:T(8,128)S(1)}, u32[]{:S(2)}, u32[]{:S(2)}) %collective-permute-start) | collective-permute-done | bytes 557088 | tf_op jit(solution)/shard_map/while/body/eval_jaxpr/ppermute | solution.py:34
  423.1 12.8 %collective-permute-done = f32[128,1088]{0,1:T(8,128)S(1)} collective-permute-done((f32[128,1088]{0,1:T(8,128)}, f32[128,1088]{0,1:T(8,128)S(1)}, u32[]{:S(2)}, u32[]{:S(2)}) %collective-permute-start) | collective-permute-done | bytes 557088 | tf_op jit(solution)/shard_map/while/body/eval_jaxpr/ppermute | solution.py:34
  463.4 13.4 %collective-permute-done = f32[128,1088]{0,1:T(8,128)S(1)} collective-permute-done((f32[128,1088]{0,1:T(8,128)}, f32[128,1088]{0,1:T(8,128)S(1)}, u32[]{:S(2)}, u32[]{:S(2)}) %collective-permute-start) | collective-permute-done | bytes 557088 | tf_op jit(solution)/shard_map/while/body/eval_jaxpr/ppermute | solution.py:34
  484.0 14.5 %collective-permute-done = f32[128,1088]{0,1:T(8,128)S(1)} collective-permute-done((f32[128,1088]{0,1:T(8,128)}, f32[128,1088]{0,1:T(8,128)S(1)}, u32[]{:S(2)}, u32[]{:S(2)}) %collective-permute-start) | collective-permute-done | bytes 557088 | tf_op jit(solution)/shard_map/while/body/eval_jaxpr/ppermute | solution.py:34
  505.9 15.7 %collective-permute-done = f32[128,1088]{0,1:T(8,128)S(1)} collective-permute-done((f32[128,1088]{0,1:T(8,128)}, f32[128,1088]{0,1:T(8,128)S(1)}, u32[]{:S(2)}, u32[]{:S(2)}) %collective-permute-start) | collective-permute-done | bytes 557088 | tf_op jit(solution)/shard_map/while/body/eval_jaxpr/ppermute | solution.py:34
  528.9 16.8 %collective-permute-done = f32[128,1088]{0,1:T(8,128)S(1)} collective-permute-done((f32[128,1088]{0,1:T(8,128)}, f32[128,1088]{0,1:T(8,128)S(1)}, u32[]{:S(2)}, u32[]{:S(2)}) %collective-permute-start) | collective-permute-done | bytes 557088 | tf_op jit(solution)/shard_map/while/body/eval_jaxpr/ppermute | solution.py:34
  553.0 17.9 %collective-permute-done = f32[128,1088]{0,1:T(8,128)S(1)} collective-permute-done((f32[128,1088]{0,1:T(8,128)}, f32[128,1088]{0,1:T(8,128)S(1)}, u32[]{:S(2)}, u32[]{:S(2)}) %collective-permute-start) | collective-permute-done | bytes 557088 | tf_op jit(solution)/shard_map/while/body/eval_jaxpr/ppermute | solution.py:34
  578.3 18.4 %collective-permute-done = f32[128,1088]{0,1:T(8,128)S(1)} collective-permute-done((f32[128,1088]{0,1:T(8,128)}, f32[128,1088]{0,1:T(8,128)S(1)}, u32[]{:S(2)}, u32[]{:S(2)}) %collective-permute-start) | collective-permute-done | bytes 557088 | tf_op jit(solution)/shard_map/while/body/eval_jaxpr/ppermute | solution.py:34
  604.0 17.6 %collective-permute-done = f32[128,1088]{0,1:T(8,128)S(1)} collective-permute-done((f32[128,1088]{0,1:T(8,128)}, f32[128,1088]{0,1:T(8,128)S(1)}, u32[]{:S(2)}, u32[]{:S(2)}) %collective-permute-start) | collective-permute-done | bytes 557088 | tf_op jit(solution)/shard_map/while/body/eval_jaxpr/ppermute | solution.py:34
  628.9 16.7 %collective-permute-done = f32[128,1088]{0,1:T(8,128)S(1)} collective-permute-done((f32[128,1088]{0,1:T(8,128)}, f32[128,1088]{0,1:T(8,128)S(1)}, u32[]{:S(2)}, u32[]{:S(2)}) %collective-permute-start) | collective-permute-done | bytes 557088 | tf_op jit(solution)/shard_map/while/body/eval_jaxpr/ppermute | solution.py:34
  653.0 15.8 %collective-permute-done = f32[128,1088]{0,1:T(8,128)S(1)} collective-permute-done((f32[128,1088]{0,1:T(8,128)}, f32[128,1088]{0,1:T(8,128)S(1)}, u32[]{:S(2)}, u32[]{:S(2)}) %collective-permute-start) | collective-permute-done | bytes 557088 | tf_op jit(solution)/shard_map/while/body/eval_jaxpr/ppermute | solution.py:34
  676.2 15.0 %collective-permute-done = f32[128,1088]{0,1:T(8,128)S(1)} collective-permute-done((f32[128,1088]{0,1:T(8,128)}, f32[128,1088]{0,1:T(8,128)S(1)}, u32[]{:S(2)}, u32[]{:S(2)}) %collective-permute-start) | collective-permute-done | bytes 557088 | tf_op jit(solution)/shard_map/while/body/eval_jaxpr/ppermute | solution.py:34
  698.5 14.1 %collective-permute-done = f32[128,1088]{0,1:T(8,128)S(1)} collective-permute-done((f32[128,1088]{0,1:T(8,128)}, f32[128,1088]{0,1:T(8,128)S(1)}, u32[]{:S(2)}, u32[]{:S(2)}) %collective-permute-start) | collective-permute-done | bytes 557088 | tf_op jit(solution)/shard_map/while/body/eval_jaxpr/ppermute | solution.py:34
  719.9 13.2 %collective-permute-done = f32[128,1088]{0,1:T(8,128)S(1)} collective-permute-done((f32[128,1088]{0,1:T(8,128)}, f32[128,1088]{0,1:T(8,128)S(1)}, u32[]{:S(2)}, u32[]{:S(2)}) %collective-permute-start) | collective-permute-done | bytes 557088 | tf_op jit(solution)/shard_map/while/body/eval_jaxpr/ppermute | solution.py:34
  780.8 12.8 %collective-permute-done = f32[128,1088]{0,1:T(8,128)S(1)} collective-permute-done((f32[128,1088]{0,1:T(8,128)}, f32[128,1088]{0,1:T(8,128)S(1)}, u32[]{:S(2)}, u32[]{:S(2)}) %collective-permute-start) | collective-permute-done | bytes 557088 | tf_op jit(solution)/shard_map/while/body/eval_jaxpr/ppermute | solution.py:34
  800.9 12.8 %collective-permute-done = f32[128,1088]{0,1:T(8,128)S(1)} collective-permute-done((f32[128,1088]{0,1:T(8,128)}, f32[128,1088]{0,1:T(8,128)S(1)}, u32[]{:S(2)}, u32[]{:S(2)}) %collective-permute-start) | collective-permute-done | bytes 557088 | tf_op jit(solution)/shard_map/while/body/eval_jaxpr/ppermute | solution.py:34
  841.1 18.2 %collective-permute-done = f32[128,1088]{0,1:T(8,128)S(1)} collective-permute-done((f32[128,1088]{0,1:T(8,128)}, f32[128,1088]{0,1:T(8,128)S(1)}, u32[]{:S(2)}, u32[]{:S(2)}) %collective-permute-start) | collective-permute-done | bytes 557088 | tf_op jit(solution)/shard_map/while/body/eval_jaxpr/ppermute | solution.py:34
  866.6 12.8 %collective-permute-done = f32[128,1088]{0,1:T(8,128)S(1)} collective-permute-done((f32[128,1088]{0,1:T(8,128)}, f32[128,1088]{0,1:T(8,128)S(1)}, u32[]{:S(2)}, u32[]{:S(2)}) %collective-permute-start) | collective-permute-done | bytes 557088 | tf_op jit(solution)/shard_map/while/body/eval_jaxpr/ppermute | solution.py:34
  886.8 16.4 %collective-permute-done = f32[128,1088]{0,1:T(8,128)S(1)} collective-permute-done((f32[128,1088]{0,1:T(8,128)}, f32[128,1088]{0,1:T(8,128)S(1)}, u32[]{:S(2)}, u32[]{:S(2)}) %collective-permute-start) | collective-permute-done | bytes 557088 | tf_op jit(solution)/shard_map/while/body/eval_jaxpr/ppermute | solution.py:34
  903.3 13.7 %collective-permute-done.1 = f32[128,1088]{0,1:T(8,128)S(1)} collective-permute-done((f32[128,1088]{0,1:T(8,128)S(1)}, f32[128,1088]{0,1:T(8,128)S(1)}, u32[]{:S(2)}, u32[]{:S(2)}) %collective-permute-start.1) | collective-permute-done | bytes 557088 | tf_op jit(solution)/shard_map/ppermute | solution.py:34
  936.9 17.7 %all-to-all-done.2 = f32[32,1,16384]{2,1,0:T(1,128)} async-done(((f32[32,1,16384]{2,1,0:T(1,128)}), f32[32,1,16384]{2,1,0:T(1,128)}, u32[]{:S(2)}, u32[]{:S(2)}) %all-to-all-start.2) | async-done | bytes 2097184 | tf_op jit(solution)/shard_map/all_to_all | solution.py:48
  963.1 14.3 %all-to-all-done.1 = f32[4,128,576]{1,2,0:T(8,128)S(1)} async-done(((f32[4,128,576]{1,2,0:T(8,128)}), f32[4,128,576]{1,2,0:T(8,128)S(1)}, u32[]{:S(2)}, u32[]{:S(2)}) %all-to-all-start.1) | async-done | bytes 1179680 | tf_op jit(solution)/shard_map/all_to_all | solution.py:22
  990.9 22.2 %all-to-all-done.3 = f32[32,1,16384]{2,1,0:T(1,128)S(1)} async-done(((f32[32,1,16384]{2,1,0:T(1,128)}), f32[32,1,16384]{2,1,0:T(1,128)S(1)}, u32[]{:S(2)}, u32[]{:S(2)}) %all-to-all-start.3) | async-done | bytes 2097184 | tf_op jit(solution)/shard_map/all_to_all | solution.py:22
  (707 shorter events, 449.8 us)
Async XLA Ops:
  7.2 145.2 %all-gather.2.cloned.1.call-start = ((), (), s32[]{:S(2)}) async-start(), calls=%async_computation.4 | async-start | bytes 4866048 | tf_op jit(solution)/shard_map/all_gather | solution.py:168
  9.2 17.6 %all-to-all-start = ((s32[32,1,128]{2,1,0:T(1,128)}), s32[32,1,128]{2,1,0:T(1,128)}, u32[]{:S(2)}, u32[]{:S(2)}) async-start(s32[32,1,128]{2,1,0:T(1,128)} %broadcast_in_dim.132), calls=%async_computation | async-start | bytes 32768 | tf_op jit(solution)/shard_map/all_to_all | solution.py:22
  232.3 17.4 %collective-permute-start = (f32[128,1088]{0,1:T(8,128)}, f32[128,1088]{0,1:T(8,128)S(1)}, u32[]{:S(2)}, u32[]{:S(2)}) collective-permute-start(f32[128,1088]{0,1:T(8,128)} %maximum_add_fusion.3), channel_id=1, source_target_pairs={{0,4},{4,8},{8,12},{12,16},{16,20},{20,24},{24,28},{28,32},{32,36}... | collective-permute-start | bytes 1671176 | tf_op jit(solution)/shard_map/while/body/eval_jaxpr/ppermute | solution.py:34
  255.8 16.6 %collective-permute-start = (f32[128,1088]{0,1:T(8,128)}, f32[128,1088]{0,1:T(8,128)S(1)}, u32[]{:S(2)}, u32[]{:S(2)}) collective-permute-start(f32[128,1088]{0,1:T(8,128)} %maximum_add_fusion.3), channel_id=1, source_target_pairs={{0,4},{4,8},{8,12},{12,16},{16,20},{20,24},{24,28},{28,32},{32,36}... | collective-permute-start | bytes 1671176 | tf_op jit(solution)/shard_map/while/body/eval_jaxpr/ppermute | solution.py:34
  278.5 15.7 %collective-permute-start = (f32[128,1088]{0,1:T(8,128)}, f32[128,1088]{0,1:T(8,128)S(1)}, u32[]{:S(2)}, u32[]{:S(2)}) collective-permute-start(f32[128,1088]{0,1:T(8,128)} %maximum_add_fusion.3), channel_id=1, source_target_pairs={{0,4},{4,8},{8,12},{12,16},{16,20},{20,24},{24,28},{28,32},{32,36}... | collective-permute-start | bytes 1671176 | tf_op jit(solution)/shard_map/while/body/eval_jaxpr/ppermute | solution.py:34
  300.4 14.9 %collective-permute-start = (f32[128,1088]{0,1:T(8,128)}, f32[128,1088]{0,1:T(8,128)S(1)}, u32[]{:S(2)}, u32[]{:S(2)}) collective-permute-start(f32[128,1088]{0,1:T(8,128)} %maximum_add_fusion.3), channel_id=1, source_target_pairs={{0,4},{4,8},{8,12},{12,16},{16,20},{20,24},{24,28},{28,32},{32,36}... | collective-permute-start | bytes 1671176 | tf_op jit(solution)/shard_map/while/body/eval_jaxpr/ppermute | solution.py:34
  321.4 14.0 %collective-permute-start = (f32[128,1088]{0,1:T(8,128)}, f32[128,1088]{0,1:T(8,128)S(1)}, u32[]{:S(2)}, u32[]{:S(2)}) collective-permute-start(f32[128,1088]{0,1:T(8,128)} %maximum_add_fusion.3), channel_id=1, source_target_pairs={{0,4},{4,8},{8,12},{12,16},{16,20},{20,24},{24,28},{28,32},{32,36}... | collective-permute-start | bytes 1671176 | tf_op jit(solution)/shard_map/while/body/eval_jaxpr/ppermute | solution.py:34
  341.5 14.0 %collective-permute-start = (f32[128,1088]{0,1:T(8,128)}, f32[128,1088]{0,1:T(8,128)S(1)}, u32[]{:S(2)}, u32[]{:S(2)}) collective-permute-start(f32[128,1088]{0,1:T(8,128)} %maximum_add_fusion.3), channel_id=1, source_target_pairs={{0,4},{4,8},{8,12},{12,16},{16,20},{20,24},{24,28},{28,32},{32,36}... | collective-permute-start | bytes 1671176 | tf_op jit(solution)/shard_map/while/body/eval_jaxpr/ppermute | solution.py:34
  361.6 14.0 %collective-permute-start = (f32[128,1088]{0,1:T(8,128)}, f32[128,1088]{0,1:T(8,128)S(1)}, u32[]{:S(2)}, u32[]{:S(2)}) collective-permute-start(f32[128,1088]{0,1:T(8,128)} %maximum_add_fusion.3), channel_id=1, source_target_pairs={{0,4},{4,8},{8,12},{12,16},{16,20},{20,24},{24,28},{28,32},{32,36}... | collective-permute-start | bytes 1671176 | tf_op jit(solution)/shard_map/while/body/eval_jaxpr/ppermute | solution.py:34
  381.7 14.0 %collective-permute-start = (f32[128,1088]{0,1:T(8,128)}, f32[128,1088]{0,1:T(8,128)S(1)}, u32[]{:S(2)}, u32[]{:S(2)}) collective-permute-start(f32[128,1088]{0,1:T(8,128)} %maximum_add_fusion.3), channel_id=1, source_target_pairs={{0,4},{4,8},{8,12},{12,16},{16,20},{20,24},{24,28},{28,32},{32,36}... | collective-permute-start | bytes 1671176 | tf_op jit(solution)/shard_map/while/body/eval_jaxpr/ppermute | solution.py:34
  401.8 14.0 %collective-permute-start = (f32[128,1088]{0,1:T(8,128)}, f32[128,1088]{0,1:T(8,128)S(1)}, u32[]{:S(2)}, u32[]{:S(2)}) collective-permute-start(f32[128,1088]{0,1:T(8,128)} %maximum_add_fusion.3), channel_id=1, source_target_pairs={{0,4},{4,8},{8,12},{12,16},{16,20},{20,24},{24,28},{28,32},{32,36}... | collective-permute-start | bytes 1671176 | tf_op jit(solution)/shard_map/while/body/eval_jaxpr/ppermute | solution.py:34
  422.0 14.0 %collective-permute-start = (f32[128,1088]{0,1:T(8,128)}, f32[128,1088]{0,1:T(8,128)S(1)}, u32[]{:S(2)}, u32[]{:S(2)}) collective-permute-start(f32[128,1088]{0,1:T(8,128)} %maximum_add_fusion.3), channel_id=1, source_target_pairs={{0,4},{4,8},{8,12},{12,16},{16,20},{20,24},{24,28},{28,32},{32,36}... | collective-permute-start | bytes 1671176 | tf_op jit(solution)/shard_map/while/body/eval_jaxpr/ppermute | solution.py:34
  442.1 14.0 %collective-permute-start = (f32[128,1088]{0,1:T(8,128)}, f32[128,1088]{0,1:T(8,128)S(1)}, u32[]{:S(2)}, u32[]{:S(2)}) collective-permute-start(f32[128,1088]{0,1:T(8,128)} %maximum_add_fusion.3), channel_id=1, source_target_pairs={{0,4},{4,8},{8,12},{12,16},{16,20},{20,24},{24,28},{28,32},{32,36}... | collective-permute-start | bytes 1671176 | tf_op jit(solution)/shard_map/while/body/eval_jaxpr/ppermute | solution.py:34
  462.2 14.5 %collective-permute-start = (f32[128,1088]{0,1:T(8,128)}, f32[128,1088]{0,1:T(8,128)S(1)}, u32[]{:S(2)}, u32[]{:S(2)}) collective-permute-start(f32[128,1088]{0,1:T(8,128)} %maximum_add_fusion.3), channel_id=1, source_target_pairs={{0,4},{4,8},{8,12},{12,16},{16,20},{20,24},{24,28},{28,32},{32,36}... | collective-permute-start | bytes 1671176 | tf_op jit(solution)/shard_map/while/body/eval_jaxpr/ppermute | solution.py:34
  482.9 15.7 %collective-permute-start = (f32[128,1088]{0,1:T(8,128)}, f32[128,1088]{0,1:T(8,128)S(1)}, u32[]{:S(2)}, u32[]{:S(2)}) collective-permute-start(f32[128,1088]{0,1:T(8,128)} %maximum_add_fusion.3), channel_id=1, source_target_pairs={{0,4},{4,8},{8,12},{12,16},{16,20},{20,24},{24,28},{28,32},{32,36}... | collective-permute-start | bytes 1671176 | tf_op jit(solution)/shard_map/while/body/eval_jaxpr/ppermute | solution.py:34
  504.7 16.8 %collective-permute-start = (f32[128,1088]{0,1:T(8,128)}, f32[128,1088]{0,1:T(8,128)S(1)}, u32[]{:S(2)}, u32[]{:S(2)}) collective-permute-start(f32[128,1088]{0,1:T(8,128)} %maximum_add_fusion.3), channel_id=1, source_target_pairs={{0,4},{4,8},{8,12},{12,16},{16,20},{20,24},{24,28},{28,32},{32,36}... | collective-permute-start | bytes 1671176 | tf_op jit(solution)/shard_map/while/body/eval_jaxpr/ppermute | solution.py:34
  527.7 18.0 %collective-permute-start = (f32[128,1088]{0,1:T(8,128)}, f32[128,1088]{0,1:T(8,128)S(1)}, u32[]{:S(2)}, u32[]{:S(2)}) collective-permute-start(f32[128,1088]{0,1:T(8,128)} %maximum_add_fusion.3), channel_id=1, source_target_pairs={{0,4},{4,8},{8,12},{12,16},{16,20},{20,24},{24,28},{28,32},{32,36}... | collective-permute-start | bytes 1671176 | tf_op jit(solution)/shard_map/while/body/eval_jaxpr/ppermute | solution.py:34
  551.8 19.1 %collective-permute-start = (f32[128,1088]{0,1:T(8,128)}, f32[128,1088]{0,1:T(8,128)S(1)}, u32[]{:S(2)}, u32[]{:S(2)}) collective-permute-start(f32[128,1088]{0,1:T(8,128)} %maximum_add_fusion.3), channel_id=1, source_target_pairs={{0,4},{4,8},{8,12},{12,16},{16,20},{20,24},{24,28},{28,32},{32,36}... | collective-permute-start | bytes 1671176 | tf_op jit(solution)/shard_map/while/body/eval_jaxpr/ppermute | solution.py:34
  577.1 19.6 %collective-permute-start = (f32[128,1088]{0,1:T(8,128)}, f32[128,1088]{0,1:T(8,128)S(1)}, u32[]{:S(2)}, u32[]{:S(2)}) collective-permute-start(f32[128,1088]{0,1:T(8,128)} %maximum_add_fusion.3), channel_id=1, source_target_pairs={{0,4},{4,8},{8,12},{12,16},{16,20},{20,24},{24,28},{28,32},{32,36}... | collective-permute-start | bytes 1671176 | tf_op jit(solution)/shard_map/while/body/eval_jaxpr/ppermute | solution.py:34
  602.9 18.7 %collective-permute-start = (f32[128,1088]{0,1:T(8,128)}, f32[128,1088]{0,1:T(8,128)S(1)}, u32[]{:S(2)}, u32[]{:S(2)}) collective-permute-start(f32[128,1088]{0,1:T(8,128)} %maximum_add_fusion.3), channel_id=1, source_target_pairs={{0,4},{4,8},{8,12},{12,16},{16,20},{20,24},{24,28},{28,32},{32,36}... | collective-permute-start | bytes 1671176 | tf_op jit(solution)/shard_map/while/body/eval_jaxpr/ppermute | solution.py:34
  627.8 17.9 %collective-permute-start = (f32[128,1088]{0,1:T(8,128)}, f32[128,1088]{0,1:T(8,128)S(1)}, u32[]{:S(2)}, u32[]{:S(2)}) collective-permute-start(f32[128,1088]{0,1:T(8,128)} %maximum_add_fusion.3), channel_id=1, source_target_pairs={{0,4},{4,8},{8,12},{12,16},{16,20},{20,24},{24,28},{28,32},{32,36}... | collective-permute-start | bytes 1671176 | tf_op jit(solution)/shard_map/while/body/eval_jaxpr/ppermute | solution.py:34
  651.8 17.0 %collective-permute-start = (f32[128,1088]{0,1:T(8,128)}, f32[128,1088]{0,1:T(8,128)S(1)}, u32[]{:S(2)}, u32[]{:S(2)}) collective-permute-start(f32[128,1088]{0,1:T(8,128)} %maximum_add_fusion.3), channel_id=1, source_target_pairs={{0,4},{4,8},{8,12},{12,16},{16,20},{20,24},{24,28},{28,32},{32,36}... | collective-permute-start | bytes 1671176 | tf_op jit(solution)/shard_map/while/body/eval_jaxpr/ppermute | solution.py:34
  675.0 16.2 %collective-permute-start = (f32[128,1088]{0,1:T(8,128)}, f32[128,1088]{0,1:T(8,128)S(1)}, u32[]{:S(2)}, u32[]{:S(2)}) collective-permute-start(f32[128,1088]{0,1:T(8,128)} %maximum_add_fusion.3), channel_id=1, source_target_pairs={{0,4},{4,8},{8,12},{12,16},{16,20},{20,24},{24,28},{28,32},{32,36}... | collective-permute-start | bytes 1671176 | tf_op jit(solution)/shard_map/while/body/eval_jaxpr/ppermute | solution.py:34
  697.3 15.3 %collective-permute-start = (f32[128,1088]{0,1:T(8,128)}, f32[128,1088]{0,1:T(8,128)S(1)}, u32[]{:S(2)}, u32[]{:S(2)}) collective-permute-start(f32[128,1088]{0,1:T(8,128)} %maximum_add_fusion.3), channel_id=1, source_target_pairs={{0,4},{4,8},{8,12},{12,16},{16,20},{20,24},{24,28},{28,32},{32,36}... | collective-permute-start | bytes 1671176 | tf_op jit(solution)/shard_map/while/body/eval_jaxpr/ppermute | solution.py:34
  718.7 14.4 %collective-permute-start = (f32[128,1088]{0,1:T(8,128)}, f32[128,1088]{0,1:T(8,128)S(1)}, u32[]{:S(2)}, u32[]{:S(2)}) collective-permute-start(f32[128,1088]{0,1:T(8,128)} %maximum_add_fusion.3), channel_id=1, source_target_pairs={{0,4},{4,8},{8,12},{12,16},{16,20},{20,24},{24,28},{28,32},{32,36}... | collective-permute-start | bytes 1671176 | tf_op jit(solution)/shard_map/while/body/eval_jaxpr/ppermute | solution.py:34
  739.3 14.0 %collective-permute-start = (f32[128,1088]{0,1:T(8,128)}, f32[128,1088]{0,1:T(8,128)S(1)}, u32[]{:S(2)}, u32[]{:S(2)}) collective-permute-start(f32[128,1088]{0,1:T(8,128)} %maximum_add_fusion.3), channel_id=1, source_target_pairs={{0,4},{4,8},{8,12},{12,16},{16,20},{20,24},{24,28},{28,32},{32,36}... | collective-permute-start | bytes 1671176 | tf_op jit(solution)/shard_map/while/body/eval_jaxpr/ppermute | solution.py:34
  759.5 14.0 %collective-permute-start = (f32[128,1088]{0,1:T(8,128)}, f32[128,1088]{0,1:T(8,128)S(1)}, u32[]{:S(2)}, u32[]{:S(2)}) collective-permute-start(f32[128,1088]{0,1:T(8,128)} %maximum_add_fusion.3), channel_id=1, source_target_pairs={{0,4},{4,8},{8,12},{12,16},{16,20},{20,24},{24,28},{28,32},{32,36}... | collective-permute-start | bytes 1671176 | tf_op jit(solution)/shard_map/while/body/eval_jaxpr/ppermute | solution.py:34
  840.0 19.3 %collective-permute-start = (f32[128,1088]{0,1:T(8,128)}, f32[128,1088]{0,1:T(8,128)S(1)}, u32[]{:S(2)}, u32[]{:S(2)}) collective-permute-start(f32[128,1088]{0,1:T(8,128)} %maximum_add_fusion.3), channel_id=1, source_target_pairs={{0,4},{4,8},{8,12},{12,16},{16,20},{20,24},{24,28},{28,32},{32,36}... | collective-permute-start | bytes 1671176 | tf_op jit(solution)/shard_map/while/body/eval_jaxpr/ppermute | solution.py:34
  885.6 17.6 %collective-permute-start = (f32[128,1088]{0,1:T(8,128)}, f32[128,1088]{0,1:T(8,128)S(1)}, u32[]{:S(2)}, u32[]{:S(2)}) collective-permute-start(f32[128,1088]{0,1:T(8,128)} %maximum_add_fusion.3), channel_id=1, source_target_pairs={{0,4},{4,8},{8,12},{12,16},{16,20},{20,24},{24,28},{28,32},{32,36}... | collective-permute-start | bytes 1671176 | tf_op jit(solution)/shard_map/while/body/eval_jaxpr/ppermute | solution.py:34
  931.2 23.4 %all-to-all-start.2 = ((f32[32,1,16384]{2,1,0:T(1,128)}), f32[32,1,16384]{2,1,0:T(1,128)}, u32[]{:S(2)}, u32[]{:S(2)}) async-start(f32[32,1,16384]{2,1,0:T(1,128)} %copy.122), calls=%async_computation.2 | async-start | bytes 4194304 | tf_op jit(solution)/shard_map/all_to_all | solution.py:48
  955.7 21.8 %all-to-all-start.1 = ((f32[4,128,576]{1,2,0:T(8,128)}), f32[4,128,576]{1,2,0:T(8,128)S(1)}, u32[]{:S(2)}, u32[]{:S(2)}) async-start(f32[4,128,576]{1,2,0:T(8,128)} %broadcast_in_dim.136), calls=%async_computation.1 | async-start | bytes 2359296 | tf_op jit(solution)/shard_map/all_to_all | solution.py:22
  980.7 32.4 %all-to-all-start.3 = ((f32[32,1,16384]{2,1,0:T(1,128)}), f32[32,1,16384]{2,1,0:T(1,128)S(1)}, u32[]{:S(2)}, u32[]{:S(2)}) async-start(f32[32,1,16384]{2,1,0:T(1,128)} %broadcast_in_dim.137), calls=%async_computation.3 | async-start | bytes 4194304 | tf_op jit(solution)/shard_map/all_to_all | solution.py:22
  (20 other events, 194.0 us)
Sparse Core Ops, SparseCore 0:
  9.5 142.7 all-gather.1
where the time goes:
time: 1040 us; the launch traced here: 1030 us
  waiting for transfers between devices  647 us (62%)
  matrix products  218 us (21%)
  local copies, waits for them, and re-layouts  63.9 us (6%)
  other arithmetic  61.2 us (6%)
  starting transfers between devices  23.4 us (2%)
  between operations  14.4 us (1%)
    ppermute x32, waiting for transfers between devices, shifted(): return lax.ppermute(value, axis, pairs)  463 us
    all_gather x1, waiting for transfers between devices, shards(): gathered = lax.all_gather(latents, 'seq', axis=0, tiled=True)  123 us
    dot_general x40, matrix products, up_project(): jnp.dot(compressed, value_up, preferred_element_type=jnp.float32)  50.9 us
    dot_general x40, matrix products, up_project(): jnp.dot(compressed, key_up, preferred_element_type=jnp.float32)  50.7 us
    all_to_all x3, waiting for transfers between devices, from_everyone(): lax.all_to_all(jnp.broadcast_to(shard[None], (size, *shard.shape)), axis,...  42.5 us
    dot_general x40, matrix products, scores_of(): jnp.einsum('bhd,kd->hbk', q_rope, rope_keys, preferred_element_type=jnp.f...  39.2 us
    add x63, other arithmetic, grad_block(): return (grads + part, q_acc + q_grad)  29.4 us
    dot_general x32, matrix products, backward_terms(): jnp.einsum('hbk,kd->bhd', dscore, rope_keys, preferred_element_type=jnp.f...  27.9 us
  transfers between devices with their start and end apart: 37, of which 37 were waited for; matrix products, arithmetic and copies ran while one was open for 5% of the time, Pallas kernels for 0%

commit v1 on v0

--- a/solution.py
+++ b/solution.py
@@ -9,6 +9,13 @@
 D_NOPE = 128
 D_V = 128
 NEG = -1e30
+
+
+def gather_over(array, name, dim):
+    count = lax.axis_size(name)
+    blocks = jnp.stack([array for _ in range(count)])
+    blocks = lax.all_to_all(blocks, name, split_axis=0, concat_axis=0)
+    return jnp.concatenate(blocks, axis=dim)
 
 
 def joined_along(tiles, dim):
@@ -165,7 +172,7 @@
         )
         return (grads + part, q_acc + q_grad)
 
-    gathered = lax.all_gather(latents, "seq", axis=0, tiled=True)
+    gathered = gather_over(latents, "seq", 0)
     count = gathered.shape[0]
     width = math.gcd(count, 512)
 

time: 1040 us -> 939 us (0.903)
  waiting for transfers between devices: 647 us -> 566 us
  other arithmetic: 61.2 us -> 28.5 us
  blocking collectives: 0 us -> 17.5 us
  between operations: 14.4 us -> 1.03 us
    all_gather x1 -> x0, waiting for transfers between devices: 123 us -> none  [shards(): gathered = lax.all_gather(latents, 'seq', axis=0, tiled=True)]
    all_to_all x0 -> x1, waiting for transfers between devices: none -> 55.6 us  [gather_over(): blocks = lax.all_to_all(blocks, name, split_axis=0, concat_axis=0)]
    add x63, other arithmetic: 29.4 us -> 5.5 us  [grad_block(): return (grads + part, q_acc + q_grad)]
    all_to_all x0 -> x1, blocking collectives: none -> 17.5 us  [from_everyone(): lax.all_to_all(jnp.broadcast_to(shard[None], (size, *shard.shape)), axis,...]
    all_to_all x3 -> x2, waiting for transfers between devices: 42.5 us -> 39.8 us  [from_everyone(): lax.all_to_all(jnp.broadcast_to(shard[None], (size, *shard.shape)), axis,...]
  transfers between devices with their start and end apart: 37 -> 36, of which waited for: 37 -> 36; matrix products, arithmetic and copies ran while one was open for 5% -> 5% of each run, Pallas kernels for 0% -> 0%
where the time goes in v1:
time: 939 us; the launch traced here: 930 us
  waiting for transfers between devices  566 us (60%)
  matrix products  226 us (24%)
  local copies, waits for them, and re-layouts  66.6 us (7%)
  other arithmetic  28.5 us (3%)
  starting transfers between devices  20.2 us (2%)
  blocking collectives  17.5 us (2%)
    ppermute x32, waiting for transfers between devices, shifted(): return lax.ppermute(value, axis, pairs)  455 us
    all_to_all x1, waiting for transfers between devices, gather_over(): blocks = lax.all_to_all(blocks, name, split_axis=0, concat_axis=0)  55.6 us
    dot_general x40, matrix products, up_project(): jnp.dot(compressed, value_up, preferred_element_type=jnp.float32)  49.8 us
    dot_general x40, matrix products, up_project(): jnp.dot(compressed, key_up, preferred_element_type=jnp.float32)  49.7 us
    all_to_all x2, waiting for transfers between devices, from_everyone(): lax.all_to_all(jnp.broadcast_to(shard[None], (size, *shard.shape)), axis,...  39.8 us
    dot_general x40, matrix products, scores_of(): jnp.einsum('bhd,kd->hbk', q_rope, rope_keys, preferred_element_type=jnp.f...  39.2 us
    dot_general x32, matrix products, backward_terms(): jnp.einsum('hbk,kd->bhd', dscore, rope_keys, preferred_element_type=jnp.f...  27.9 us
    dynamic_slice x32, local copies, waits for them, and re-layouts, owner_pos(): return lax.dynamic_slice_in_dim(every_pos, owner_start(step), rows, 0)  24.2 us
  transfers between devices with their start and end apart: 36, of which 36 were waited for; matrix products, arithmetic and copies ran while one was open for 5% of the time, Pallas kernels for 0%

profile of v1, /device:TPU:0, one launch (start us, length us, event | category | flops | bytes accessed | tf_op | source)
XLA Modules:
  0.0 930.4 jit_solution(15934401266809863371)
XLA Ops:
  1.3 17.5 %all_to_all.31 = s32[32,1,128]{2,1,0:T(1,128)} all-to-all(s32[32,1,128]{2,1,0:T(1,128)S(1)} %broadcast_in_dim.132), channel_id=1, replica_groups=mesh['seq'=32,'head'=4] {'seq'}, dimensions={0} | all-to-all | bytes 32768 | tf_op jit(solution)/shard_map/all_to_all | solution.py:29
  29.8 55.6 %all-to-all-done.1 = bf16[32,128,576]{1,2,0:T(8,128)(2,1)} async-done(((bf16[32,128,576]{1,2,0:T(8,128)(2,1)}), bf16[32,128,576]{1,2,0:T(8,128)(2,1)}, u32[]{:S(2)}, u32[]{:S(2)}) %all-to-all-start.1) | async-done | bytes 4718624 | tf_op jit(solution)/shard_map/all_to_all | solution.py:17
  93.4 66.3 %while.36 = (s32[]{:T(128)}, f32[4,128]{1,0:T(4,128)S(1)}, f32[4,128]{1,0:T(4,128)S(1)}, f32[4,128]{1,0:T(4,128)}, s32[4096]{0:T(1024)}, /*index=5*/s32[128]{0:T...) while((s32[]{:T(128)}, f32[4,128]{1,0:T(4,128)S(1)}, ...), condition=%wide.region_4.5_spmd.clone, body=%wide.region_0.4_spmd.clone.sunk | while | flops 708120064 | bytes 10136302 | solution.py:183
  165.6 647.2 %while.37 = (s32[]{:T(128)}, f32[128,1088]{0,1:T(8,128)S(1)}, f32[128,768]{0,1:T(8,128)}, s32[]{:T(128)}, s32[4096]{0:T(1024)}, /*index=5*/s32[128]{0:T(128)S(1)...) while((s32[]{:T(128)}, f32[128,1088]{0,1:T(8,128)S(1)}, ...), condition=%wide.region_6.7_spmd.clone, body=%wide.region_5.6_spmd.clone.sunk | while | flops 244719632 | bytes 14883310 | solution.py:194
  172.3 14.7 %collective-permute-done = f32[128,1088]{0,1:T(8,128)S(1)} collective-permute-done((f32[128,1088]{0,1:T(8,128)S(1)}, f32[128,1088]{0,1:T(8,128)S(1)}, u32[]{:S(2)}, u32[]{:S(2)}) %collective-permute-start) | collective-permute-done | bytes 557088 | tf_op jit(solution)/shard_map/while/body/eval_jaxpr/ppermute | solution.py:41
  193.7 13.8 %collective-permute-done = f32[128,1088]{0,1:T(8,128)S(1)} collective-permute-done((f32[128,1088]{0,1:T(8,128)S(1)}, f32[128,1088]{0,1:T(8,128)S(1)}, u32[]{:S(2)}, u32[]{:S(2)}) %collective-permute-start) | collective-permute-done | bytes 557088 | tf_op jit(solution)/shard_map/while/body/eval_jaxpr/ppermute | solution.py:41
  214.2 13.0 %collective-permute-done = f32[128,1088]{0,1:T(8,128)S(1)} collective-permute-done((f32[128,1088]{0,1:T(8,128)S(1)}, f32[128,1088]{0,1:T(8,128)S(1)}, u32[]{:S(2)}, u32[]{:S(2)}) %collective-permute-start) | collective-permute-done | bytes 557088 | tf_op jit(solution)/shard_map/while/body/eval_jaxpr/ppermute | solution.py:41
  233.8 12.5 %collective-permute-done = f32[128,1088]{0,1:T(8,128)S(1)} collective-permute-done((f32[128,1088]{0,1:T(8,128)S(1)}, f32[128,1088]{0,1:T(8,128)S(1)}, u32[]{:S(2)}, u32[]{:S(2)}) %collective-permute-start) | collective-permute-done | bytes 557088 | tf_op jit(solution)/shard_map/while/body/eval_jaxpr/ppermute | solution.py:41
  253.1 12.5 %collective-permute-done = f32[128,1088]{0,1:T(8,128)S(1)} collective-permute-done((f32[128,1088]{0,1:T(8,128)S(1)}, f32[128,1088]{0,1:T(8,128)S(1)}, u32[]{:S(2)}, u32[]{:S(2)}) %collective-permute-start) | collective-permute-done | bytes 557088 | tf_op jit(solution)/shard_map/while/body/eval_jaxpr/ppermute | solution.py:41
  272.3 12.5 %collective-permute-done = f32[128,1088]{0,1:T(8,128)S(1)} collective-permute-done((f32[128,1088]{0,1:T(8,128)S(1)}, f32[128,1088]{0,1:T(8,128)S(1)}, u32[]{:S(2)}, u32[]{:S(2)}) %collective-permute-start) | collective-permute-done | bytes 557088 | tf_op jit(solution)/shard_map/while/body/eval_jaxpr/ppermute | solution.py:41
  330.0 12.6 %collective-permute-done = f32[128,1088]{0,1:T(8,128)S(1)} collective-permute-done((f32[128,1088]{0,1:T(8,128)S(1)}, f32[128,1088]{0,1:T(8,128)S(1)}, u32[]{:S(2)}, u32[]{:S(2)}) %collective-permute-start) | collective-permute-done | bytes 557088 | tf_op jit(solution)/shard_map/while/body/eval_jaxpr/ppermute | solution.py:41
  349.2 13.7 %collective-permute-done = f32[128,1088]{0,1:T(8,128)S(1)} collective-permute-done((f32[128,1088]{0,1:T(8,128)S(1)}, f32[128,1088]{0,1:T(8,128)S(1)}, u32[]{:S(2)}, u32[]{:S(2)}) %collective-permute-start) | collective-permute-done | bytes 557088 | tf_op jit(solution)/shard_map/while/body/eval_jaxpr/ppermute | solution.py:41
  369.7 14.9 %collective-permute-done = f32[128,1088]{0,1:T(8,128)S(1)} collective-permute-done((f32[128,1088]{0,1:T(8,128)S(1)}, f32[128,1088]{0,1:T(8,128)S(1)}, u32[]{:S(2)}, u32[]{:S(2)}) %collective-permute-start) | collective-permute-done | bytes 557088 | tf_op jit(solution)/shard_map/while/body/eval_jaxpr/ppermute | solution.py:41
  391.2 16.0 %collective-permute-done = f32[128,1088]{0,1:T(8,128)S(1)} collective-permute-done((f32[128,1088]{0,1:T(8,128)S(1)}, f32[128,1088]{0,1:T(8,128)S(1)}, u32[]{:S(2)}, u32[]{:S(2)}) %collective-permute-start) | collective-permute-done | bytes 557088 | tf_op jit(solution)/shard_map/while/body/eval_jaxpr/ppermute | solution.py:41
  413.9 17.2 %collective-permute-done = f32[128,1088]{0,1:T(8,128)S(1)} collective-permute-done((f32[128,1088]{0,1:T(8,128)S(1)}, f32[128,1088]{0,1:T(8,128)S(1)}, u32[]{:S(2)}, u32[]{:S(2)}) %collective-permute-start) | collective-permute-done | bytes 557088 | tf_op jit(solution)/shard_map/while/body/eval_jaxpr/ppermute | solution.py:41
  437.8 18.3 %collective-permute-done = f32[128,1088]{0,1:T(8,128)S(1)} collective-permute-done((f32[128,1088]{0,1:T(8,128)S(1)}, f32[128,1088]{0,1:T(8,128)S(1)}, u32[]{:S(2)}, u32[]{:S(2)}) %collective-permute-start) | collective-permute-done | bytes 557088 | tf_op jit(solution)/shard_map/while/body/eval_jaxpr/ppermute | solution.py:41
  462.8 17.6 %collective-permute-done = f32[128,1088]{0,1:T(8,128)S(1)} collective-permute-done((f32[128,1088]{0,1:T(8,128)S(1)}, f32[128,1088]{0,1:T(8,128)S(1)}, u32[]{:S(2)}, u32[]{:S(2)}) %collective-permute-start) | collective-permute-done | bytes 557088 | tf_op jit(solution)/shard_map/while/body/eval_jaxpr/ppermute | solution.py:41
  487.1 16.8 %collective-permute-done = f32[128,1088]{0,1:T(8,128)S(1)} collective-permute-done((f32[128,1088]{0,1:T(8,128)S(1)}, f32[128,1088]{0,1:T(8,128)S(1)}, u32[]{:S(2)}, u32[]{:S(2)}) %collective-permute-start) | collective-permute-done | bytes 557088 | tf_op jit(solution)/shard_map/while/body/eval_jaxpr/ppermute | solution.py:41
  510.6 15.9 %collective-permute-done = f32[128,1088]{0,1:T(8,128)S(1)} collective-permute-done((f32[128,1088]{0,1:T(8,128)S(1)}, f32[128,1088]{0,1:T(8,128)S(1)}, u32[]{:S(2)}, u32[]{:S(2)}) %collective-permute-start) | collective-permute-done | bytes 557088 | tf_op jit(solution)/shard_map/while/body/eval_jaxpr/ppermute | solution.py:41
  533.2 15.1 %collective-permute-done = f32[128,1088]{0,1:T(8,128)S(1)} collective-permute-done((f32[128,1088]{0,1:T(8,128)S(1)}, f32[128,1088]{0,1:T(8,128)S(1)}, u32[]{:S(2)}, u32[]{:S(2)}) %collective-permute-start) | collective-permute-done | bytes 557088 | tf_op jit(solution)/shard_map/while/body/eval_jaxpr/ppermute | solution.py:41
  555.0 14.2 %collective-permute-done = f32[128,1088]{0,1:T(8,128)S(1)} collective-permute-done((f32[128,1088]{0,1:T(8,128)S(1)}, f32[128,1088]{0,1:T(8,128)S(1)}, u32[]{:S(2)}, u32[]{:S(2)}) %collective-permute-start) | collective-permute-done | bytes 557088 | tf_op jit(solution)/shard_map/while/body/eval_jaxpr/ppermute | solution.py:41
  575.9 13.4 %collective-permute-done = f32[128,1088]{0,1:T(8,128)S(1)} collective-permute-done((f32[128,1088]{0,1:T(8,128)S(1)}, f32[128,1088]{0,1:T(8,128)S(1)}, u32[]{:S(2)}, u32[]{:S(2)}) %collective-permute-start) | collective-permute-done | bytes 557088 | tf_op jit(solution)/shard_map/while/body/eval_jaxpr/ppermute | solution.py:41
  615.2 12.5 %collective-permute-done = f32[128,1088]{0,1:T(8,128)S(1)} collective-permute-done((f32[128,1088]{0,1:T(8,128)S(1)}, f32[128,1088]{0,1:T(8,128)S(1)}, u32[]{:S(2)}, u32[]{:S(2)}) %collective-permute-start) | collective-permute-done | bytes 557088 | tf_op jit(solution)/shard_map/while/body/eval_jaxpr/ppermute | solution.py:41
  711.4 13.3 %collective-permute-done = f32[128,1088]{0,1:T(8,128)S(1)} collective-permute-done((f32[128,1088]{0,1:T(8,128)S(1)}, f32[128,1088]{0,1:T(8,128)S(1)}, u32[]{:S(2)}, u32[]{:S(2)}) %collective-permute-start) | collective-permute-done | bytes 557088 | tf_op jit(solution)/shard_map/while/body/eval_jaxpr/ppermute | solution.py:41
  731.4 14.5 %collective-permute-done = f32[128,1088]{0,1:T(8,128)S(1)} collective-permute-done((f32[128,1088]{0,1:T(8,128)S(1)}, f32[128,1088]{0,1:T(8,128)S(1)}, u32[]{:S(2)}, u32[]{:S(2)}) %collective-permute-start) | collective-permute-done | bytes 557088 | tf_op jit(solution)/shard_map/while/body/eval_jaxpr/ppermute | solution.py:41
  752.6 15.6 %collective-permute-done = f32[128,1088]{0,1:T(8,128)S(1)} collective-permute-done((f32[128,1088]{0,1:T(8,128)S(1)}, f32[128,1088]{0,1:T(8,128)S(1)}, u32[]{:S(2)}, u32[]{:S(2)}) %collective-permute-start) | collective-permute-done | bytes 557088 | tf_op jit(solution)/shard_map/while/body/eval_jaxpr/ppermute | solution.py:41
  774.9 16.0 %collective-permute-done = f32[128,1088]{0,1:T(8,128)S(1)} collective-permute-done((f32[128,1088]{0,1:T(8,128)S(1)}, f32[128,1088]{0,1:T(8,128)S(1)}, u32[]{:S(2)}, u32[]{:S(2)}) %collective-permute-start) | collective-permute-done | bytes 557088 | tf_op jit(solution)/shard_map/while/body/eval_jaxpr/ppermute | solution.py:41
  797.5 15.2 %collective-permute-done = f32[128,1088]{0,1:T(8,128)S(1)} collective-permute-done((f32[128,1088]{0,1:T(8,128)S(1)}, f32[128,1088]{0,1:T(8,128)S(1)}, u32[]{:S(2)}, u32[]{:S(2)}) %collective-permute-start) | collective-permute-done | bytes 557088 | tf_op jit(solution)/shard_map/while/body/eval_jaxpr/ppermute | solution.py:41
  813.9 15.1 %collective-permute-done.1 = f32[128,1088]{0,1:T(8,128)S(1)} collective-permute-done((f32[128,1088]{0,1:T(8,128)S(1)}, f32[128,1088]{0,1:T(8,128)S(1)}, u32[]{:S(2)}, u32[]{:S(2)}) %collective-permute-start.1) | collective-permute-done | bytes 557088 | tf_op jit(solution)/shard_map/ppermute | solution.py:41
  846.3 15.6 %all-to-all-done.3 = f32[32,1,16384]{2,1,0:T(1,128)S(1)} async-done(((f32[32,1,16384]{2,1,0:T(1,128)}), f32[32,1,16384]{2,1,0:T(1,128)S(1)}, u32[]{:S(2)}, u32[]{:S(2)}) %all-to-all-start.3) | async-done | bytes 2097184 | tf_op jit(solution)/shard_map/all_to_all | solution.py:55
  868.8 16.0 %all-to-all-done.2 = f32[4,128,576]{1,2,0:T(8,128)} async-done(((f32[4,128,576]{1,2,0:T(8,128)}), f32[4,128,576]{1,2,0:T(8,128)}, u32[]{:S(2)}, u32[]{:S(2)}) %all-to-all-start.2) | async-done | bytes 1179680 | tf_op jit(solution)/shard_map/all_to_all | solution.py:29
  896.6 23.8 %all-to-all-done.4 = f32[32,1,16384]{2,1,0:T(1,128)S(1)} async-done(((f32[32,1,16384]{2,1,0:T(1,128)}), f32[32,1,16384]{2,1,0:T(1,128)S(1)}, u32[]{:S(2)}, u32[]{:S(2)}) %all-to-all-start.4) | async-done | bytes 2097184 | tf_op jit(solution)/shard_map/all_to_all | solution.py:29
  (826 shorter events, 429.5 us)
Async XLA Ops:
  23.0 62.4 %all-to-all-start.1 = ((bf16[32,128,576]{1,2,0:T(8,128)(2,1)}), bf16[32,128,576]{1,2,0:T(8,128)(2,1)}, u32[]{:S(2)}, u32[]{:S(2)}) async-start(bf16[32,128,576]{1,2,0:T(8,128)(2,1)} %stack.2), calls=%async_computation.1 | async-start | bytes 9437184 | tf_op jit(solution)/shard_map/all_to_all | solution.py:17
  171.0 16.0 %collective-permute-start = (f32[128,1088]{0,1:T(8,128)S(1)}, f32[128,1088]{0,1:T(8,128)S(1)}, u32[]{:S(2)}, u32[]{:S(2)}) collective-permute-start(f32[128,1088]{0,1:T(8,128)S(1)} %maximum_add_fusion.3), channel_id=1, source_target_pairs={{0,4},{4,8},{8,12},{12,16},{16,20},{20,24},{24,28},{28,32},{32,36}... | collective-permute-start | bytes 1671176 | tf_op jit(solution)/shard_map/while/body/eval_jaxpr/ppermute | solution.py:41
  192.4 15.1 %collective-permute-start = (f32[128,1088]{0,1:T(8,128)S(1)}, f32[128,1088]{0,1:T(8,128)S(1)}, u32[]{:S(2)}, u32[]{:S(2)}) collective-permute-start(f32[128,1088]{0,1:T(8,128)S(1)} %maximum_add_fusion.3), channel_id=1, source_target_pairs={{0,4},{4,8},{8,12},{12,16},{16,20},{20,24},{24,28},{28,32},{32,36}... | collective-permute-start | bytes 1671176 | tf_op jit(solution)/shard_map/while/body/eval_jaxpr/ppermute | solution.py:41
  212.9 14.2 %collective-permute-start = (f32[128,1088]{0,1:T(8,128)S(1)}, f32[128,1088]{0,1:T(8,128)S(1)}, u32[]{:S(2)}, u32[]{:S(2)}) collective-permute-start(f32[128,1088]{0,1:T(8,128)S(1)} %maximum_add_fusion.3), channel_id=1, source_target_pairs={{0,4},{4,8},{8,12},{12,16},{16,20},{20,24},{24,28},{28,32},{32,36}... | collective-permute-start | bytes 1671176 | tf_op jit(solution)/shard_map/while/body/eval_jaxpr/ppermute | solution.py:41
  232.5 13.8 %collective-permute-start = (f32[128,1088]{0,1:T(8,128)S(1)}, f32[128,1088]{0,1:T(8,128)S(1)}, u32[]{:S(2)}, u32[]{:S(2)}) collective-permute-start(f32[128,1088]{0,1:T(8,128)S(1)} %maximum_add_fusion.3), channel_id=1, source_target_pairs={{0,4},{4,8},{8,12},{12,16},{16,20},{20,24},{24,28},{28,32},{32,36}... | collective-permute-start | bytes 1671176 | tf_op jit(solution)/shard_map/while/body/eval_jaxpr/ppermute | solution.py:41
  251.8 13.8 %collective-permute-start = (f32[128,1088]{0,1:T(8,128)S(1)}, f32[128,1088]{0,1:T(8,128)S(1)}, u32[]{:S(2)}, u32[]{:S(2)}) collective-permute-start(f32[128,1088]{0,1:T(8,128)S(1)} %maximum_add_fusion.3), channel_id=1, source_target_pairs={{0,4},{4,8},{8,12},{12,16},{16,20},{20,24},{24,28},{28,32},{32,36}... | collective-permute-start | bytes 1671176 | tf_op jit(solution)/shard_map/while/body/eval_jaxpr/ppermute | solution.py:41
  271.0 13.8 %collective-permute-start = (f32[128,1088]{0,1:T(8,128)S(1)}, f32[128,1088]{0,1:T(8,128)S(1)}, u32[]{:S(2)}, u32[]{:S(2)}) collective-permute-start(f32[128,1088]{0,1:T(8,128)S(1)} %maximum_add_fusion.3), channel_id=1, source_target_pairs={{0,4},{4,8},{8,12},{12,16},{16,20},{20,24},{24,28},{28,32},{32,36}... | collective-permute-start | bytes 1671176 | tf_op jit(solution)/shard_map/while/body/eval_jaxpr/ppermute | solution.py:41
  290.2 13.8 %collective-permute-start = (f32[128,1088]{0,1:T(8,128)S(1)}, f32[128,1088]{0,1:T(8,128)S(1)}, u32[]{:S(2)}, u32[]{:S(2)}) collective-permute-start(f32[128,1088]{0,1:T(8,128)S(1)} %maximum_add_fusion.3), channel_id=1, source_target_pairs={{0,4},{4,8},{8,12},{12,16},{16,20},{20,24},{24,28},{28,32},{32,36}... | collective-permute-start | bytes 1671176 | tf_op jit(solution)/shard_map/while/body/eval_jaxpr/ppermute | solution.py:41
  309.5 13.8 %collective-permute-start = (f32[128,1088]{0,1:T(8,128)S(1)}, f32[128,1088]{0,1:T(8,128)S(1)}, u32[]{:S(2)}, u32[]{:S(2)}) collective-permute-start(f32[128,1088]{0,1:T(8,128)S(1)} %maximum_add_fusion.3), channel_id=1, source_target_pairs={{0,4},{4,8},{8,12},{12,16},{16,20},{20,24},{24,28},{28,32},{32,36}... | collective-permute-start | bytes 1671176 | tf_op jit(solution)/shard_map/while/body/eval_jaxpr/ppermute | solution.py:41
  328.7 13.9 %collective-permute-start = (f32[128,1088]{0,1:T(8,128)S(1)}, f32[128,1088]{0,1:T(8,128)S(1)}, u32[]{:S(2)}, u32[]{:S(2)}) collective-permute-start(f32[128,1088]{0,1:T(8,128)S(1)} %maximum_add_fusion.3), channel_id=1, source_target_pairs={{0,4},{4,8},{8,12},{12,16},{16,20},{20,24},{24,28},{28,32},{32,36}... | collective-permute-start | bytes 1671176 | tf_op jit(solution)/shard_map/while/body/eval_jaxpr/ppermute | solution.py:41
  348.0 15.0 %collective-permute-start = (f32[128,1088]{0,1:T(8,128)S(1)}, f32[128,1088]{0,1:T(8,128)S(1)}, u32[]{:S(2)}, u32[]{:S(2)}) collective-permute-start(f32[128,1088]{0,1:T(8,128)S(1)} %maximum_add_fusion.3), channel_id=1, source_target_pairs={{0,4},{4,8},{8,12},{12,16},{16,20},{20,24},{24,28},{28,32},{32,36}... | collective-permute-start | bytes 1671176 | tf_op jit(solution)/shard_map/while/body/eval_jaxpr/ppermute | solution.py:41
  368.4 16.2 %collective-permute-start = (f32[128,1088]{0,1:T(8,128)S(1)}, f32[128,1088]{0,1:T(8,128)S(1)}, u32[]{:S(2)}, u32[]{:S(2)}) collective-permute-start(f32[128,1088]{0,1:T(8,128)S(1)} %maximum_add_fusion.3), channel_id=1, source_target_pairs={{0,4},{4,8},{8,12},{12,16},{16,20},{20,24},{24,28},{28,32},{32,36}... | collective-permute-start | bytes 1671176 | tf_op jit(solution)/shard_map/while/body/eval_jaxpr/ppermute | solution.py:41
  389.9 17.3 %collective-permute-start = (f32[128,1088]{0,1:T(8,128)S(1)}, f32[128,1088]{0,1:T(8,128)S(1)}, u32[]{:S(2)}, u32[]{:S(2)}) collective-permute-start(f32[128,1088]{0,1:T(8,128)S(1)} %maximum_add_fusion.3), channel_id=1, source_target_pairs={{0,4},{4,8},{8,12},{12,16},{16,20},{20,24},{24,28},{28,32},{32,36}... | collective-permute-start | bytes 1671176 | tf_op jit(solution)/shard_map/while/body/eval_jaxpr/ppermute | solution.py:41
  412.6 18.4 %collective-permute-start = (f32[128,1088]{0,1:T(8,128)S(1)}, f32[128,1088]{0,1:T(8,128)S(1)}, u32[]{:S(2)}, u32[]{:S(2)}) collective-permute-start(f32[128,1088]{0,1:T(8,128)S(1)} %maximum_add_fusion.3), channel_id=1, source_target_pairs={{0,4},{4,8},{8,12},{12,16},{16,20},{20,24},{24,28},{28,32},{32,36}... | collective-permute-start | bytes 1671176 | tf_op jit(solution)/shard_map/while/body/eval_jaxpr/ppermute | solution.py:41
  436.5 19.6 %collective-permute-start = (f32[128,1088]{0,1:T(8,128)S(1)}, f32[128,1088]{0,1:T(8,128)S(1)}, u32[]{:S(2)}, u32[]{:S(2)}) collective-permute-start(f32[128,1088]{0,1:T(8,128)S(1)} %maximum_add_fusion.3), channel_id=1, source_target_pairs={{0,4},{4,8},{8,12},{12,16},{16,20},{20,24},{24,28},{28,32},{32,36}... | collective-permute-start | bytes 1671176 | tf_op jit(solution)/shard_map/while/body/eval_jaxpr/ppermute | solution.py:41
  461.5 18.9 %collective-permute-start = (f32[128,1088]{0,1:T(8,128)S(1)}, f32[128,1088]{0,1:T(8,128)S(1)}, u32[]{:S(2)}, u32[]{:S(2)}) collective-permute-start(f32[128,1088]{0,1:T(8,128)S(1)} %maximum_add_fusion.3), channel_id=1, source_target_pairs={{0,4},{4,8},{8,12},{12,16},{16,20},{20,24},{24,28},{28,32},{32,36}... | collective-permute-start | bytes 1671176 | tf_op jit(solution)/shard_map/while/body/eval_jaxpr/ppermute | solution.py:41
  485.8 18.1 %collective-permute-start = (f32[128,1088]{0,1:T(8,128)S(1)}, f32[128,1088]{0,1:T(8,128)S(1)}, u32[]{:S(2)}, u32[]{:S(2)}) collective-permute-start(f32[128,1088]{0,1:T(8,128)S(1)} %maximum_add_fusion.3), channel_id=1, source_target_pairs={{0,4},{4,8},{8,12},{12,16},{16,20},{20,24},{24,28},{28,32},{32,36}... | collective-permute-start | bytes 1671176 | tf_op jit(solution)/shard_map/while/body/eval_jaxpr/ppermute | solution.py:41
  509.3 17.2 %collective-permute-start = (f32[128,1088]{0,1:T(8,128)S(1)}, f32[128,1088]{0,1:T(8,128)S(1)}, u32[]{:S(2)}, u32[]{:S(2)}) collective-permute-start(f32[128,1088]{0,1:T(8,128)S(1)} %maximum_add_fusion.3), channel_id=1, source_target_pairs={{0,4},{4,8},{8,12},{12,16},{16,20},{20,24},{24,28},{28,32},{32,36}... | collective-permute-start | bytes 1671176 | tf_op jit(solution)/shard_map/while/body/eval_jaxpr/ppermute | solution.py:41
  531.9 16.4 %collective-permute-start = (f32[128,1088]{0,1:T(8,128)S(1)}, f32[128,1088]{0,1:T(8,128)S(1)}, u32[]{:S(2)}, u32[]{:S(2)}) collective-permute-start(f32[128,1088]{0,1:T(8,128)S(1)} %maximum_add_fusion.3), channel_id=1, source_target_pairs={{0,4},{4,8},{8,12},{12,16},{16,20},{20,24},{24,28},{28,32},{32,36}... | collective-permute-start | bytes 1671176 | tf_op jit(solution)/shard_map/while/body/eval_jaxpr/ppermute | solution.py:41
  553.7 15.5 %collective-permute-start = (f32[128,1088]{0,1:T(8,128)S(1)}, f32[128,1088]{0,1:T(8,128)S(1)}, u32[]{:S(2)}, u32[]{:S(2)}) collective-permute-start(f32[128,1088]{0,1:T(8,128)S(1)} %maximum_add_fusion.3), channel_id=1, source_target_pairs={{0,4},{4,8},{8,12},{12,16},{16,20},{20,24},{24,28},{28,32},{32,36}... | collective-permute-start | bytes 1671176 | tf_op jit(solution)/shard_map/while/body/eval_jaxpr/ppermute | solution.py:41
  574.7 14.7 %collective-permute-start = (f32[128,1088]{0,1:T(8,128)S(1)}, f32[128,1088]{0,1:T(8,128)S(1)}, u32[]{:S(2)}, u32[]{:S(2)}) collective-permute-start(f32[128,1088]{0,1:T(8,128)S(1)} %maximum_add_fusion.3), channel_id=1, source_target_pairs={{0,4},{4,8},{8,12},{12,16},{16,20},{20,24},{24,28},{28,32},{32,36}... | collective-permute-start | bytes 1671176 | tf_op jit(solution)/shard_map/while/body/eval_jaxpr/ppermute | solution.py:41
  594.7 13.8 %collective-permute-start = (f32[128,1088]{0,1:T(8,128)S(1)}, f32[128,1088]{0,1:T(8,128)S(1)}, u32[]{:S(2)}, u32[]{:S(2)}) collective-permute-start(f32[128,1088]{0,1:T(8,128)S(1)} %maximum_add_fusion.3), channel_id=1, source_target_pairs={{0,4},{4,8},{8,12},{12,16},{16,20},{20,24},{24,28},{28,32},{32,36}... | collective-permute-start | bytes 1671176 | tf_op jit(solution)/shard_map/while/body/eval_jaxpr/ppermute | solution.py:41
  614.0 13.8 %collective-permute-start = (f32[128,1088]{0,1:T(8,128)S(1)}, f32[128,1088]{0,1:T(8,128)S(1)}, u32[]{:S(2)}, u32[]{:S(2)}) collective-permute-start(f32[128,1088]{0,1:T(8,128)S(1)} %maximum_add_fusion.3), channel_id=1, source_target_pairs={{0,4},{4,8},{8,12},{12,16},{16,20},{20,24},{24,28},{28,32},{32,36}... | collective-permute-start | bytes 1671176 | tf_op jit(solution)/shard_map/while/body/eval_jaxpr/ppermute | solution.py:41
  710.1 14.6 %collective-permute-start = (f32[128,1088]{0,1:T(8,128)S(1)}, f32[128,1088]{0,1:T(8,128)S(1)}, u32[]{:S(2)}, u32[]{:S(2)}) collective-permute-start(f32[128,1088]{0,1:T(8,128)S(1)} %maximum_add_fusion.3), channel_id=1, source_target_pairs={{0,4},{4,8},{8,12},{12,16},{16,20},{20,24},{24,28},{28,32},{32,36}... | collective-permute-start | bytes 1671176 | tf_op jit(solution)/shard_map/while/body/eval_jaxpr/ppermute | solution.py:41
  730.1 15.8 %collective-permute-start = (f32[128,1088]{0,1:T(8,128)S(1)}, f32[128,1088]{0,1:T(8,128)S(1)}, u32[]{:S(2)}, u32[]{:S(2)}) collective-permute-start(f32[128,1088]{0,1:T(8,128)S(1)} %maximum_add_fusion.3), channel_id=1, source_target_pairs={{0,4},{4,8},{8,12},{12,16},{16,20},{20,24},{24,28},{28,32},{32,36}... | collective-permute-start | bytes 1671176 | tf_op jit(solution)/shard_map/while/body/eval_jaxpr/ppermute | solution.py:41
  751.3 16.9 %collective-permute-start = (f32[128,1088]{0,1:T(8,128)S(1)}, f32[128,1088]{0,1:T(8,128)S(1)}, u32[]{:S(2)}, u32[]{:S(2)}) collective-permute-start(f32[128,1088]{0,1:T(8,128)S(1)} %maximum_add_fusion.3), channel_id=1, source_target_pairs={{0,4},{4,8},{8,12},{12,16},{16,20},{20,24},{24,28},{28,32},{32,36}... | collective-permute-start | bytes 1671176 | tf_op jit(solution)/shard_map/while/body/eval_jaxpr/ppermute | solution.py:41
  773.6 17.3 %collective-permute-start = (f32[128,1088]{0,1:T(8,128)S(1)}, f32[128,1088]{0,1:T(8,128)S(1)}, u32[]{:S(2)}, u32[]{:S(2)}) collective-permute-start(f32[128,1088]{0,1:T(8,128)S(1)} %maximum_add_fusion.3), channel_id=1, source_target_pairs={{0,4},{4,8},{8,12},{12,16},{16,20},{20,24},{24,28},{28,32},{32,36}... | collective-permute-start | bytes 1671176 | tf_op jit(solution)/shard_map/while/body/eval_jaxpr/ppermute | solution.py:41
  796.2 16.5 %collective-permute-start = (f32[128,1088]{0,1:T(8,128)S(1)}, f32[128,1088]{0,1:T(8,128)S(1)}, u32[]{:S(2)}, u32[]{:S(2)}) collective-permute-start(f32[128,1088]{0,1:T(8,128)S(1)} %maximum_add_fusion.3), channel_id=1, source_target_pairs={{0,4},{4,8},{8,12},{12,16},{16,20},{20,24},{24,28},{28,32},{32,36}... | collective-permute-start | bytes 1671176 | tf_op jit(solution)/shard_map/while/body/eval_jaxpr/ppermute | solution.py:41
  813.9 15.2 %collective-permute-start.1 = (f32[128,1088]{0,1:T(8,128)S(1)}, f32[128,1088]{0,1:T(8,128)S(1)}, u32[]{:S(2)}, u32[]{:S(2)}) collective-permute-start(f32[128,1088]{0,1:T(8,128)S(1)} %maximum_add_fusion.1), channel_id=1, source_target_pairs={{0,4},{4,8},{8,12},{12,16},{16,20},{20,24},{24,28},{28,32},{32,36}... | collective-permute-start | bytes 1671176 | tf_op jit(solution)/shard_map/ppermute | solution.py:41
  839.3 22.6 %all-to-all-start.3 = ((f32[32,1,16384]{2,1,0:T(1,128)}), f32[32,1,16384]{2,1,0:T(1,128)S(1)}, u32[]{:S(2)}, u32[]{:S(2)}) async-start(f32[32,1,16384]{2,1,0:T(1,128)} %copy.123), calls=%async_computation.3 | async-start | bytes 4194304 | tf_op jit(solution)/shard_map/all_to_all | solution.py:55
  863.1 21.7 %all-to-all-start.2 = ((f32[4,128,576]{1,2,0:T(8,128)}), f32[4,128,576]{1,2,0:T(8,128)}, u32[]{:S(2)}, u32[]{:S(2)}) async-start(f32[4,128,576]{1,2,0:T(8,128)} %broadcast_in_dim.136), calls=%async_computation.2 | async-start | bytes 2359296 | tf_op jit(solution)/shard_map/all_to_all | solution.py:29
  888.0 32.4 %all-to-all-start.4 = ((f32[32,1,16384]{2,1,0:T(1,128)}), f32[32,1,16384]{2,1,0:T(1,128)S(1)}, u32[]{:S(2)}, u32[]{:S(2)}) async-start(f32[32,1,16384]{2,1,0:T(1,128)} %broadcast_in_dim.137), calls=%async_computation.4 | async-start | bytes 4194304 | tf_op jit(solution)/shard_map/all_to_all | solution.py:29
  (79 other events, 946.0 us)
